TPU v7x, 32 devices: a whole 2x2x4 slice. The times are simulated.
32 devices in a mesh: dop: 8 (over z, y), slow: 4 (over x, core).
Axes of the slice: x: 2, y: 2, z: 4, core: 2. Of those that a mesh axis runs over, the one named last changes fastest.
Arguments:
- profiles: bfloat16 [32, 2, 1024, 2048], P('slow', None, 'dop'), may hold values from -6 to 6
- range_walk: int32 [2048], replicated, may hold values from -32 to 32
- band_order: int32 [32], replicated, may hold values from 0 to 31, each once
Outputs:
- ambiguity: float32 [2048, 1024], P(('dop', 'slow'))
Inputs may be any that keep to these rules, and one draw needn't show every extreme that they name: `band_order`: each band number appears exactly once.
All inputs are finite; a program needn't handle non-finite values.
Results may differ from a plain program's by a relative error of at most 0.00067.
Values sent between devices are 32-bit elements; how exact they have to be, the bound alone decides.
A program may use at most 128 MiB of HBM per device.

v0:
```python
import math

import jax
import jax.numpy as jnp
from jax import lax
from jax.sharding import PartitionSpec as P

WALK = 32


def from_behind(value, axis, steps):
    count = lax.axis_size(axis)
    leading, last = (max(0, -steps), min(count, count - steps))
    return lax.ppermute(value, axis, [(source, source + steps) for source in range(leading, last)])


def fourier_tables(length):
    counter = jnp.arange(length, dtype=jnp.int32)
    phases = counter[:, None] * counter[None, :] % length
    angles = phases.astype(jnp.float32) * (2.0 * math.pi / length)
    return (jnp.cos(angles).astype(jnp.bfloat16), jnp.sin(angles).astype(jnp.bfloat16))


def batch_powers(block, cosine, sine_table):
    count = block.shape[0]
    delays = block.shape[2]
    bins = block.shape[3]
    stacked = block.reshape(count * 2 * delays, bins)
    first = jnp.dot(stacked, cosine, preferred_element_type=jnp.float32).reshape(
        count, 2, delays, bins
    )
    second = jnp.dot(stacked, sine_table, preferred_element_type=jnp.float32).reshape(
        count, 2, delays, bins
    )
    real_part = first[:, 0] + second[:, 1]
    imag_part = first[:, 1] - second[:, 0]
    return real_part * real_part + imag_part * imag_part


def walk_align(padded, offsets, out_rows, reach):
    moves = offsets + reach
    levels = max(1, (2 * reach).bit_length())
    needed = out_rows + (1 << levels) - 1
    current = jnp.pad(padded, ((0, 0), (0, needed - padded.shape[1]), (0, 0)))
    for level in range(levels):
        stride = 1 << level
        taken = (moves // stride % 2 == 1)[:, None, :]
        current = jnp.where(taken, current[:, stride:], current[:, :-stride])
    return current


def permute_bands(values, band_order, band_count):
    picker = (band_order[:, None] == jnp.arange(band_count, dtype=jnp.int32)[None, :]).astype(
        jnp.float32
    )
    return jnp.einsum("bc,...cj->...bj", picker, values, precision=lax.Precision.HIGHEST)


def on_device(profiles, range_walk, band_order):
    batch_count = profiles.shape[0]
    local_rows = profiles.shape[2]
    doppler_bins = profiles.shape[3]
    dop_count = lax.axis_size("dop")
    slow_count = lax.axis_size("slow")
    total_batches = batch_count * slow_count
    band_count = dop_count * slow_count
    band_rows = doppler_bins // band_count
    scale = 1.0 / (total_batches * doppler_bins)
    cosine, sine_table = fourier_tables(doppler_bins)
    powers = batch_powers(profiles, cosine, sine_table)
    batches = lax.axis_index("slow") * batch_count + jnp.arange(batch_count, dtype=jnp.int32)
    offsets = range_walk[None, :] * batches[:, None] // total_batches
    widened = jnp.pad(powers, ((0, 0), (2 * WALK, 2 * WALK), (0, 0)))
    gathered = jnp.sum(walk_align(widened, offsets, local_rows + 2 * WALK, WALK), axis=0)
    lower_rim = gathered[:WALK]
    upper_rim = gathered[local_rows + WALK :]
    own_rows = gathered[WALK : local_rows + WALK]
    from_below = from_behind(upper_rim, "dop", 1)
    from_above = from_behind(lower_rim, "dop", -1)
    own_rows = own_rows.at[:WALK].add(from_below)
    own_rows = own_rows.at[local_rows - WALK :].add(from_above)
    partial_value = own_rows * scale
    ordered = permute_bands(
        partial_value.reshape(local_rows, band_count, band_rows), band_order, band_count
    )
    grouped = ordered.reshape(local_rows, dop_count, slow_count, band_rows).transpose(0, 2, 1, 3)
    grouped = grouped.reshape(local_rows, doppler_bins)
    summed = lax.psum_scatter(grouped, "slow", scatter_dimension=1, tiled=True)
    result = lax.all_to_all(summed, "dop", split_axis=1, concat_axis=0, tiled=True)
    return result.T


def solution(mesh):
    placed = (P("slow", None, "dop", None), P(), P())
    return jax.shard_map(
        on_device, mesh=mesh, in_specs=placed, out_specs=P(("dop", "slow"), None), check_vma=False
    )
```

profile of v0, /device:TPU:0, one launch (start us, length us, event | category | flops | bytes accessed | tf_op | source)
XLA Modules:
  0.0 317.6 jit_solution(7998774098427603306)
XLA Ops:
  6.5 0.0 reduce-scatter.2.cloned.1.call-start
  6.5 0.0 slice-start
  6.5 61.8 %sine_convert_fusion.4 = bf16[2048,2048]{1,0:T(8,128)(2,1)S(1)} fusion(), kind=kLoop, calls=%fused_computation.14.clone.clone.1 | loop fusion | flops 62914560 | bytes 8388608 | tf_op jit(solution)/shard_map/dot_general | solution.py:32
  68.4 0.0 slice-start.1
  68.4 61.3 %cosine_convert_fusion.4 = bf16[2048,2048]{1,0:T(8,128)(2,1)S(1)} fusion(), kind=kLoop, calls=%fused_computation.15.clone.clone.1 | loop fusion | flops 62914560 | bytes 8388608 | tf_op jit(solution)/shard_map/dot_general | solution.py:29
  129.7 0.0 slice-done
  129.7 0.0 slice-done.1
  129.7 20.6 %fusion.9 = f32[2048,2048]{0,1:T(8,128)} fusion(bf16[2048,2048]{1,0:T(8,128)(2,1)S(1)} %bitcast.68, bf16[2048,2048]{1,0:T(8,128)(2,1)S(1)} %sine_convert_fusion.4), kind=kOutput, calls=%fused_computation.22 | convolution fusion | flops 17179869184 | bytes 33554432 | tf_op jit(solution)/shard_map/dot_general | solution.py:32
  150.2 20.5 %fusion.8 = f32[2048,2048]{0,1:T(8,128)} fusion(bf16[2048,2048]{1,0:T(8,128)(2,1)S(1)} %bitcast.69, bf16[2048,2048]{1,0:T(8,128)(2,1)S(1)} %cosine_convert_fusion.4), kind=kOutput, calls=%fused_computation.21 | convolution fusion | flops 17179869184 | bytes 33554432 | tf_op jit(solution)/shard_map/dot_general | solution.py:29
  170.8 0.0 copy-start
  170.8 12.6 %fusion.13 = f32[8,128,2048]{2,1,0:T(8,128)S(1)} fusion(f32[8,2,128,2048]{3,2,1,0:T(8,128)} %bitcast.60, f32[8,2,128,2048]{3,2,1,0:T(8,128)} %bitcast.61), kind=kLoop, calls=%fused_computation.27 | loop fusion | flops 10485760 | bytes 41943040 | tf_op jit(solution)/shard_map/add | solution.py:37
  183.5 0.0 copy-done
  183.5 0.5 fusion.26
  184.0 3.7 %fusion = f32[8,318,2048]{2,1,0:T(8,128)S(1)} fusion(f32[8,128,2048]{2,1,0:T(8,128)S(1)} %fusion.13, pred[8,2048]{1,0:T(8,128)(4,1)S(1)} %get-tuple-element.35), kind=kLoop, calls=%fused_computation.5 | loop fusion | flops 5210112 | bytes 29245440 | tf_op jit(solution)/shard_map/jit(_where)/select_n | solution.py:48
  187.7 7.8 %slice_select_fusion = f32[8,316,2048]{2,1,0:T(8,128)} fusion(f32[8,318,2048]{2,1,0:T(8,128)S(1)} %fusion, pred[8,2048]{1,0:T(8,128)(4,1)S(1)} %get-tuple-element.36), kind=kLoop, calls=%fused_computation.6 | loop fusion | flops 5177344 | bytes 62144512 | tf_op jit(solution)/shard_map/jit(_where)/select_n | solution.py:48
  195.5 14.8 %slice_select_fusion.1 = f32[8,312,2048]{2,1,0:T(8,128)S(1)} fusion(f32[8,316,2048]{2,1,0:T(8,128)} %slice_select_fusion, pred[8,2048]{1,0:T(8,128)(4,1)S(1)} %get-tuple-element.33), kind=kLoop, calls=%fused_computation.7 | loop fusion | flops 5111808 | bytes 61358080 | tf_op jit(solution)/shard_map/jit(_where)/select_n | solution.py:48
  210.3 8.2 %slice_select_fusion.2 = f32[8,304,2048]{2,1,0:T(8,128)} fusion(f32[8,312,2048]{2,1,0:T(8,128)S(1)} %slice_select_fusion.1, pred[8,2048]{1,0:T(8,128)(4,1)S(1)} %get-tuple-element.37), kind=kLoop, calls=%fused_computation.8 | loop fusion | flops 4980736 | bytes 59785216 | tf_op jit(solution)/shard_map/jit(_where)/select_n | solution.py:48
  218.5 13.4 %slice_select_fusion.3 = f32[8,288,2048]{2,1,0:T(8,128)S(1)} fusion(f32[8,304,2048]{2,1,0:T(8,128)} %slice_select_fusion.2, pred[8,2048]{1,0:T(8,128)(4,1)S(1)} %get-tuple-element.34), kind=kLoop, calls=%fused_computation.9 | loop fusion | flops 4718592 | bytes 56639488 | tf_op jit(solution)/shard_map/jit(_where)/select_n | solution.py:48
  231.9 7.8 %slice_select_fusion.4 = f32[8,256,2048]{2,1,0:T(8,128)} fusion(f32[8,288,2048]{2,1,0:T(8,128)S(1)} %slice_select_fusion.3, pred[8,2048]{1,0:T(8,128)(4,1)S(1)} %get-tuple-element.32), kind=kLoop, calls=%fused_computation.13 | loop fusion | flops 4194304 | bytes 50348032 | tf_op jit(solution)/shard_map/jit(_where)/select_n | solution.py:48
  239.7 0.0 copy-start.1
  239.7 9.5 %fusion.7 = f32[192,2048]{1,0:T(8,128)S(1)} fusion(f32[8,256,2048]{2,1,0:T(8,128)} %slice_select_fusion.4, pred[8,2048]{1,0:T(8,128)(4,1)S(1)} %get-tuple-element.31), kind=kLoop, calls=%fused_computation.20 | loop fusion | flops 5898240 | bytes 26755072 | tf_op jit(solution)/shard_map/reduce_sum | solution.py:74
  249.3 4.9 %collective-permute-start = (f32[32,2048]{1,0:T(8,128)S(1)}, f32[32,2048]{1,0:T(8,128)S(1)}, u32[]{:S(2)}, u32[]{:S(2)}) collective-permute-start(f32[32,2048]{1,0:T(8,128)S(1)} %get-tuple-element.30), channel_id=1, source_target_pairs={{0,4},{4,8},{8,12},{12,16},{16,20},{20,24},{24,28},{1,5},{5,9},{9,... | collective-permute-start | bytes 786440 | tf_op jit(solution)/shard_map/ppermute | solution.py:14
  254.2 1.3 collective-permute-start.1
  255.5 0.1 slice.141
  255.6 9.8 %collective-permute-done = f32[32,2048]{1,0:T(8,128)S(1)} collective-permute-done((f32[32,2048]{1,0:T(8,128)S(1)}, f32[32,2048]{1,0:T(8,128)S(1)}, u32[]{:S(2)}, u32[]{:S(2)}) %collective-permute-start) | collective-permute-done | bytes 262176 | tf_op jit(solution)/shard_map/ppermute | solution.py:14
  265.4 0.0 collective-permute-done.1
  265.4 0.1 fusion.20
  265.4 0.1 broadcast_multiply_fusion
  265.5 0.3 copy.13
  265.9 0.0 copy-done.1
  265.9 1.3 fusion.18
  267.2 1.6 copy.15
  268.7 0.0 reduce-scatter.2.cloned.1.call-update
  268.8 27.0 %reduce-scatter.2.cloned.1.call-done = f32[128,512]{0,1:T(8,128)} async-done(((f32[128,2048]{0,1:T(8,128)}), f32[128,512]{0,1:T(8,128)}) %reduce-scatter.2.cloned.1.call-update) | async-done | bytes 262160 | tf_op jit(solution)/shard_map/reduce_scatter | solution.py:88
  295.8 14.3 %all_to_all.19 = f32[128,8,64]{0,2,1:T(8,128)S(1)} all-to-all(f32[128,8,64]{0,2,1:T(8,128)} %bitcast.65), channel_id=1, replica_groups=mesh['dop'=8,'slow'=4] {'dop'}, dimensions={1} | all-to-all | bytes 524288 | tf_op jit(solution)/shard_map/all_to_all | solution.py:89
  310.0 0.7 bitcast_bitcast_fusion
  (4 shorter events, 0.1 us)
Async XLA Ops:
  6.5 289.2 %reduce-scatter.2.cloned.1.call-start = ((), (), s32[]{:S(2)}) async-start(), calls=%async_computation.2 | async-start | bytes 1310720 | tf_op jit(solution)/shard_map/reduce_scatter | solution.py:88
  6.5 123.1 %slice-start = ((s8[8388608]{0:T(1024)(128)(4,1)}), s8[4194304]{0:T(1024)(128)(4,1)S(1)}, s32[]{:S(2)}) async-start(s8[8388608]{0:T(1024)(128)(4,1)} %bitcast.66), calls=%async_computation.3 | async-start | bytes 8388608
  68.4 61.3 %slice-start.1 = ((s8[8388608]{0:T(1024)(128)(4,1)}), s8[4194304]{0:T(1024)(128)(4,1)S(1)}, s32[]{:S(2)}) async-start(s8[8388608]{0:T(1024)(128)(4,1)} %bitcast.66), calls=%async_computation.4 | async-start | bytes 8388608
  170.8 12.7 %copy-start = (s32[2048]{0:T(1024)S(1)}, s32[2048]{0:T(1024)}, u32[]{:S(2)}) copy-start(s32[2048]{0:T(1024)} %param.8) | copy-start | bytes 24580
  239.7 26.1 %copy-start.1 = (s32[32]{0:T(128)S(1)}, s32[32]{0:T(128)}, u32[]{:S(2)}) copy-start(s32[32]{0:T(128)} %param.9) | copy-start | bytes 388
  249.3 16.1 %collective-permute-start = (f32[32,2048]{1,0:T(8,128)S(1)}, f32[32,2048]{1,0:T(8,128)S(1)}, u32[]{:S(2)}, u32[]{:S(2)}) collective-permute-start(f32[32,2048]{1,0:T(8,128)S(1)} %get-tuple-element.30), channel_id=1, source_target_pairs={{0,4},{4,8},{8,12},{12,16},{16,20},{20,24},{24,28},{1,5},{5,9},{9,... | collective-permute-start | bytes 786440 | tf_op jit(solution)/shard_map/ppermute | solution.py:14
  254.2 11.2 %collective-permute-start.1 = (f32[32,2048]{1,0:T(8,128)S(1)}, f32[32,2048]{1,0:T(8,128)S(1)}, u32[]{:S(2)}, u32[]{:S(2)}) collective-permute-start(f32[32,2048]{1,0:T(8,128)S(1)} %get-tuple-element.29), channel_id=1, source_target_pairs={{4,0},{8,4},{12,8},{16,12},{20,16},{24,20},{28,24},{5,1},{9,5},{13... | collective-permute-start | bytes 786440 | tf_op jit(solution)/shard_map/ppermute | solution.py:14
Sparse Core Ops, SparseCore 0:
  268.9 26.8 reduce-scatter.1
where the time goes:
time: 318 us
  other arithmetic  202 us (64%)
  matrix products  42.4 us (13%)
  waiting for transfers between devices  36.8 us (12%)
  blocking collectives  14.3 us (4%)
  between operations  13.6 us (4%)
  starting transfers between devices  6.21 us (2%)
    dot_general x1, other arithmetic, batch_powers(): jnp.dot(stacked, sine_table, preferred_element_type=jnp.float32)  61.8 us
    dot_general x1, other arithmetic, batch_powers(): jnp.dot(stacked, cosine, preferred_element_type=jnp.float32)  61.3 us
    select_n x6, other arithmetic, walk_align(): current = jnp.where(taken, current[:, stride:], current[:, :-stride])  55.7 us
    reduce_scatter x1, waiting for transfers between devices, on_device(): summed = lax.psum_scatter(grouped, 'slow', scatter_dimension=1, tiled=True)  27 us
    dot_general x1, matrix products, batch_powers(): jnp.dot(stacked, sine_table, preferred_element_type=jnp.float32)  20.6 us
    dot_general x1, matrix products, batch_powers(): jnp.dot(stacked, cosine, preferred_element_type=jnp.float32)  20.5 us
    all_to_all x1, blocking collectives, on_device(): lax.all_to_all(summed, 'dop', split_axis=1, concat_axis=0, tiled=True)  14.3 us
    add x1, other arithmetic, batch_powers(): return real_part * real_part + imag_part * imag_part  12.6 us
  transfers between devices with their start and end apart: 3, of which 2 were waited for; matrix products, arithmetic and copies ran while one was open for 0% of the time, Pallas kernels for 0%

commit v1 on v0

v1 whole, which is shorter than its diff:
```python
import functools
import math

import jax
import jax.numpy as jnp
import numpy as np
from jax import lax
from jax.experimental import pallas as pl
from jax.experimental.pallas import tpu as pltpu
from jax.sharding import PartitionSpec as P

WALK = 32
LANES = 128
TILE = 16
RADIX = 4


def rotation(rows, pulses, length):
    phases = (np.asarray(rows)[..., None] * np.arange(pulses)) % length
    angles = phases * (2.0 * math.pi / length)
    return np.cos(angles).astype(np.float32), np.sin(angles).astype(np.float32)


def quarter_sums(x_ref, short):
    re = [x_ref[0, 0, :, q * short:(q + 1) * short].astype(jnp.float32) for q in range(RADIX)]
    im = [x_ref[0, 1, :, q * short:(q + 1) * short].astype(jnp.float32) for q in range(RADIX)]
    are, aim, bre, bim = re[0] + re[2], im[0] + im[2], re[0] - re[2], im[0] - im[2]
    cre, cim, dre, dim = re[1] + re[3], im[1] + im[3], re[1] - re[3], im[1] - im[3]
    return (
        (are + cre, aim + cim),
        (bre + dim, bim - dre),
        (are - cre, aim - cim),
        (bre - dim, bim + dre),
    )


def power_kernel(
    batch_count, total_batches, per_band, scale,
    order_ref, x_ref, walk_ref, base_cos, base_sin, band_cos, band_sin,
    own_ref, rim_ref, table, packed, own_sum, rim_sum,
):
    step = pl.program_id(0)
    short = x_ref.shape[3] // RADIX
    bins = table.shape[1]

    @pl.when(step == 0)
    def _():
        own_sum[...] = jnp.zeros_like(own_sum)
        rim_sum[...] = jnp.zeros_like(rim_sum)
        row = lax.broadcasted_iota(jnp.int32, (TILE, short), 0) // min(per_band, TILE)

        @pl.loop(0, bins // TILE)
        def _(tile):
            start = pl.multiple_of(tile * TILE, TILE)
            first = start // per_band
            inside = pl.multiple_of(start % per_band, TILE) if per_band > TILE else 0
            vc = band_cos[pl.ds(order_ref[first], 1), :]
            vs = band_sin[pl.ds(order_ref[first], 1), :]
            for extra in range(1, max(1, TILE // per_band)):
                band = order_ref[first + extra]
                vc = jnp.where(row == extra, band_cos[pl.ds(band, 1), :], vc)
                vs = jnp.where(row == extra, band_sin[pl.ds(band, 1), :], vs)
            for r in range(RADIX):
                bc = base_cos[r, pl.ds(inside, TILE), :]
                bs = base_sin[r, pl.ds(inside, TILE), :]
                table[r, pl.ds(start, TILE), :short] = (bc * vc - bs * vs).astype(jnp.bfloat16)
                table[r, pl.ds(start, TILE), short:] = (bs * vc + bc * vs).astype(jnp.bfloat16)

    batch = lax.axis_index("slow") * batch_count + step
    lane = lax.broadcasted_iota(jnp.int32, (bins, LANES), 1)
    sums = quarter_sums(x_ref, short)
    for r in range(RADIX):
        yre, yim = (part.astype(jnp.bfloat16) for part in sums[r])
        packed[r, :LANES, :short] = yre
        packed[r, :LANES, short:] = yim
        packed[r, LANES:, :short] = yim
        packed[r, LANES:, short:] = -yre
    for r in range(RADIX):
        spec = lax.dot_general(
            table[r], packed[r], (((1,), (1,)), ((), ())), preferred_element_type=jnp.float32
        )
        re, im = spec[:, :LANES], spec[:, LANES:]
        power = re * re + im * im
        moved = walk_ref[r] * batch
        if total_batches & (total_batches - 1) == 0:
            offset = lax.shift_right_arithmetic(moved, total_batches.bit_length() - 1)
        else:
            offset = jnp.floor_divide(moved, total_batches)
        source = lane + offset
        wrapped = source & (LANES - 1)
        value = jnp.take_along_axis(power, wrapped, axis=1, mode="promise_in_bounds")
        inside = source == wrapped
        own_sum[r] += jnp.where(inside, value, 0.0)
        rim_sum[r] += jnp.where(inside, 0.0, value)

    @pl.when(step == batch_count - 1)
    def _():
        for r in range(RADIX):
            own_ref[pl.ds(r, bins, stride=RADIX), :] = own_sum[r] * scale
            rim_ref[pl.ds(r, bins, stride=RADIX), :] = rim_sum[r] * scale


def aligned_power(profiles, range_walk, band_order, total_batches):
    batch_count, _, delays, pulses = profiles.shape
    band_count = band_order.shape[0]
    band_rows = pulses // band_count
    per_band = band_rows // RADIX
    bins, short = pulses // RADIX, pulses // RADIX
    scale = 1.0 / (total_batches * pulses)
    if delays < LANES:
        profiles = jnp.pad(profiles, ((0, 0), (0, 0), (0, LANES - delays), (0, 0)))
    picked = band_order[:, None, None] == jnp.arange(band_count, dtype=jnp.int32)[None, :, None]
    walks = jnp.sum(jnp.where(picked, range_walk.reshape(1, band_count, band_rows), 0), axis=1)
    walks = jnp.broadcast_to(walks.reshape(bins, RADIX).T[:, :, None], (RADIX, bins, LANES))
    inner = np.arange(max(per_band, TILE)) % per_band
    base = rotation(RADIX * inner[None, :] + np.arange(RADIX)[:, None], short, pulses)
    band = rotation(np.arange(band_count) * band_rows, short, pulses)
    whole = lambda shape: pl.BlockSpec(shape, lambda g, order: (0,) * len(shape))
    out = jax.ShapeDtypeStruct((pulses, LANES), jnp.float32)
    return pl.pallas_call(
        functools.partial(power_kernel, batch_count, total_batches, per_band, scale),
        out_shape=(out, out),
        grid_spec=pltpu.PrefetchScalarGridSpec(
            num_scalar_prefetch=1,
            grid=(batch_count,),
            in_specs=[
                pl.BlockSpec((1, 2, LANES, pulses), lambda g, order: (g, 0, 0, 0)),
                whole(walks.shape),
                whole(base[0].shape), whole(base[1].shape),
                whole(band[0].shape), whole(band[1].shape),
            ],
            out_specs=(whole(out.shape), whole(out.shape)),
            scratch_shapes=[
                pltpu.VMEM((RADIX, bins, 2 * short), jnp.bfloat16),
                pltpu.VMEM((RADIX, 2 * LANES, 2 * short), jnp.bfloat16),
                pltpu.VMEM((RADIX, bins, LANES), jnp.float32),
                pltpu.VMEM((RADIX, bins, LANES), jnp.float32),
            ],
        ),
        compiler_params=pltpu.CompilerParams(
            dimension_semantics=("arbitrary",), vmem_limit_bytes=48 << 20
        ),
    )(band_order, profiles, walks, *(jnp.asarray(part) for part in (*base, *band)))


def neighbours(value, steps):
    count = lax.axis_size("dop")
    pairs = [(source, source + steps) for source in range(count) if 0 <= source + steps < count]
    return lax.ppermute(value, "dop", pairs)


def exchange(own, rim, delays):
    dop_count, slow_count = lax.axis_size("dop"), lax.axis_size("slow")
    rows = own.shape[0] // (dop_count * slow_count)
    after = rim[:, :WALK] if delays == LANES else own[:, delays:delays + WALK]
    from_below = neighbours(after, 1)
    from_above = neighbours(rim[:, LANES - WALK:], -1)
    own = own[:, :delays].at[:, :WALK].add(from_below)
    own = own.at[:, delays - WALK:].add(from_above)
    grouped = own.reshape(dop_count, slow_count, rows, delays)
    summed = lax.psum_scatter(grouped, "slow", scatter_dimension=1, tiled=False)
    gathered = lax.all_to_all(summed, "dop", split_axis=0, concat_axis=0, tiled=True)
    return gathered.transpose(1, 0, 2).reshape(rows, dop_count * delays)


def on_device(profiles, range_walk, band_order):
    total_batches = profiles.shape[0] * lax.axis_size("slow")
    delays = profiles.shape[2]
    own, rim = aligned_power(profiles, range_walk, band_order, total_batches)
    return exchange(own, rim, delays)


def solution(mesh):
    placed = (P("slow", None, "dop", None), P(), P())
    return jax.shard_map(
        on_device, mesh=mesh, in_specs=placed, out_specs=P(("dop", "slow"), None), check_vma=False
    )
```

time: 318 us -> 123 us (0.39)
  other arithmetic: 202 us -> 2.68 us
  matrix products: 42.4 us -> 0 us
  local copies, waits for them, and re-layouts: 2.75 us -> 23.3 us
  Pallas kernels: 0 us -> 17.3 us
  waiting for transfers between devices: 36.8 us -> 46.2 us
    dot_general x2 -> x0, other arithmetic: 123 us -> none  [the longest x1 61.8 us: batch_powers(): jnp.dot(stacked, sine_table, preferred_element_type=jnp.float32)]
    select_n x6 -> x0, other arithmetic: 55.7 us -> none  [walk_align(): current = jnp.where(taken, current[:, stride:], current[:, :-stride])]
    dot_general x3 -> x0, matrix products: 42.4 us -> none  [the longest x1 20.6 us: batch_powers(): jnp.dot(stacked, sine_table, preferred_element_type=jnp.float32)]
    unnamed x1 -> x2, waiting for transfers between devices: 0.02 us -> 36.9 us
    reduce_scatter x1 -> x0, waiting for transfers between devices: 27 us -> none  [on_device(): summed = lax.psum_scatter(grouped, 'slow', scatter_dimension=1, tiled=True)]
    pallas_call x0 -> x1, Pallas kernels: none -> 17.3 us  [aligned_power(): pl.pallas_call(functools.partial(power_kernel, batch_count, total_batches...]
    add x2 -> x1, other arithmetic: 12.6 us -> 0.34 us  [exchange(): own = own.at[:, delays - WALK:].add(from_above)]
    scatter-add x0 -> x2, local copies, waits for them, and re-layouts: none -> 10.6 us  [the longest x1 6.08 us: exchange(): own = own.at[:, delays - WALK:].add(from_above)]
  transfers between devices with their start and end apart: 3 -> 3, of which waited for: 2 -> 2; matrix products, arithmetic and copies ran while one was open for 0% -> 6% of each run, Pallas kernels for 0% -> 0%
where the time goes in v1:
time: 123 us
  waiting for transfers between devices  46.2 us (38%)
  local copies, waits for them, and re-layouts  23.3 us (19%)
  Pallas kernels  17.3 us (14%)
  blocking collectives  13.8 us (11%)
  between operations  13.5 us (11%)
  starting transfers between devices  6.2 us (5%)
  other arithmetic  2.68 us (2%)
    unnamed x2, waiting for transfers between devices  36.9 us
    pallas_call x1, Pallas kernels, aligned_power(): pl.pallas_call(functools.partial(power_kernel, batch_count, total_batches...  17.3 us
    all_to_all x1, blocking collectives, exchange(): lax.all_to_all(summed, 'dop', split_axis=0, concat_axis=0, tiled=True)  13.8 us
    ppermute x2, waiting for transfers between devices, neighbours(): return lax.ppermute(value, 'dop', pairs)  9.21 us
    ppermute x2, starting transfers between devices, neighbours(): return lax.ppermute(value, 'dop', pairs)  6.19 us
    scatter-add x1, local copies, waits for them, and re-layouts, exchange(): own = own.at[:, delays - WALK:].add(from_above)  6.08 us
    unnamed x15, local copies, waits for them, and re-layouts  5.75 us
    scatter-add x1, local copies, waits for them, and re-layouts, exchange(): own = own[:, :delays].at[:, :WALK].add(from_below)  4.53 us
  transfers between devices with their start and end apart: 3, of which 2 were waited for; matrix products, arithmetic and copies ran while one was open for 6% of the time, Pallas kernels for 0%

profile of v1, /device:TPU:0, one launch (start us, length us, event | category | flops | bytes accessed | tf_op | source)
XLA Modules:
  0.0 123.0 jit_solution(16357663114604611688)
XLA Ops:
  6.5 0.0 all-reduce.3.cloned.1.call-start
  6.5 0.8 broadcast_in_dim.31
  7.3 0.7 iota_compare_fusion
  8.0 0.2 select_reduce_fusion
  8.3 0.2 reshape.86
  8.4 0.1 copy.22
  8.5 0.3 broadcast_in_dim.34.walk_ref
  8.9 0.0 copy-start.1
  8.9 0.9 copy-done.1
  9.8 0.0 copy-start.2
  9.8 0.9 copy-done.2
  10.7 0.0 copy-start.3
  10.7 0.8 copy-done.3
  11.5 0.0 copy-start.4
  11.5 0.8 copy-done.4
  12.4 0.0 copy-start.5
  12.4 0.7 copy-done.5
  13.0 17.3 %shard_map.73 = (f32[2048,128]{1,0:T(8,128)S(1)}, f32[2048,128]{1,0:T(8,128)S(1)}) custom-call(s32[32]{0:T(128)S(1)} %copy-done.5, bf16[8,2,128,2048]{3,2,1,0:T(8,128)(2,1)} %x_ref.1, s32[4,512,128]{2,1,0:T(8,128)S(1)} %broadcast_in_dim.34.walk_ref, f32[4,16,512]{2,1,0:T(8,128)S(1)} %copy-done.1, f32[4,16,512]{2,1,0:T(8,128)S(1)} %copy-done.2, ...), custom_call_target="tpu_custom_call" | custom-call | tf_op jit(solution)/shard_map/pallas_call | solution.py:120
  30.3 0.3 fusion
  30.7 0.0 copy-start.6
  30.7 1.0 copy.23
  31.7 4.9 %collective-permute-start = (f32[2048,32]{0,1:T(8,128)}, f32[2048,32]{0,1:T(8,128)S(1)}, u32[]{:S(2)}, u32[]{:S(2)}) collective-permute-start(f32[2048,32]{0,1:T(8,128)} %copy.23), channel_id=1, source_target_pairs={{0,4},{4,8},{8,12},{12,16},{16,20},{20,24},{24,28},{1,5},{5,9},{9,... | collective-permute-start | bytes 786440 | tf_op jit(solution)/shard_map/ppermute | solution.py:149
  36.6 0.3 copy.25
  36.9 1.3 %collective-permute-start.1 = (f32[2048,32]{0,1:T(8,128)S(1)}, f32[2048,32]{0,1:T(8,128)}, u32[]{:S(2)}, u32[]{:S(2)}) collective-permute-start(f32[2048,32]{0,1:T(8,128)S(1)} %copy.25), channel_id=1, source_target_pairs={{4,0},{8,4},{12,8},{16,12},{20,16},{24,20},{28,24},{5,1},{9,5},{13... | collective-permute-start | bytes 786440 | tf_op jit(solution)/shard_map/ppermute | solution.py:149
  38.2 0.7 compare_reduce_fusion
  38.8 9.2 %collective-permute-done = f32[2048,32]{0,1:T(8,128)S(1)} collective-permute-done((f32[2048,32]{0,1:T(8,128)}, f32[2048,32]{0,1:T(8,128)S(1)}, u32[]{:S(2)}, u32[]{:S(2)}) %collective-permute-start) | collective-permute-done | bytes 262176 | tf_op jit(solution)/shard_map/ppermute | solution.py:149
  48.1 0.3 copy.24
  48.4 0.7 add_select_fusion
  49.1 4.5 %scatter-add.6 = f32[2048,128]{1,0:T(8,128)S(1)} dynamic-update-slice(f32[2048,128]{1,0:T(8,128)S(1)} %get-tuple-element.31, f32[2048,32]{1,0:T(8,128)S(1)} %add_select_fusion, s32[]{:T(128)} %constant.62.clone.1, s32[]{:T(128)} %constant.62.clone.1) | dynamic-update-slice | bytes 524292 | tf_op jit(solution)/shard_map/scatter-add | solution.py:158
  53.7 0.0 collective-permute-done.1
  53.7 1.3 %copy.26 = f32[2048,32]{1,0:T(8,128)S(1)} copy(f32[2048,32]{0,1:T(8,128)} %collective-permute-done.1) | data formatting | bytes 524288 | tf_op jit(solution)/shard_map/ppermute | solution.py:149
  55.0 0.3 slice_add_fusion
  55.3 6.1 %scatter-add.9 = f32[2048,128]{1,0:T(8,128)S(1)} dynamic-update-slice(f32[2048,128]{1,0:T(8,128)S(1)} %scatter-add.6, f32[2048,32]{1,0:T(8,128)S(1)} %slice_add_fusion, s32[]{:T(128)} %constant.62.clone.1, s32[]{:T(128)} %constant.63.clone.1) | dynamic-update-slice | bytes 524292 | tf_op jit(solution)/shard_map/scatter-add | solution.py:159
  61.4 0.0 copy-start
  61.4 1.0 copy-done
  62.4 0.0 all-reduce.3.cloned.1.call-update
  62.5 0.0 copy-done.6
  62.5 0.6 dynamic-slice.16
  63.0 36.9 %all-reduce.3.cloned.1.call-done = f32[8,4,64,128]{3,2,1,0:T(8,128)} async-done(((f32[8,4,64,128]{3,2,1,0:T(8,128)}), f32[8,4,64,128]{3,2,1,0:T(8,128)}) %all-reduce.3.cloned.1.call-update) | async-done | bytes 1048592
  100.0 1.6 %dynamic-slice_bitcast_fusion = f32[8,64,128]{2,1,0:T(8,128)S(1)} fusion(f32[8,4,64,128]{3,2,1,0:T(8,128)} %all-reduce.3.cloned.1.call-done, u32[]{:T(128)} %bitcast.8), kind=kLoop, calls=%fused_computation.4 | loop fusion | bytes 524292 | tf_op jit(solution)/shard_map/reduce_scatter | solution.py:161
  101.6 13.8 %all_to_all.5 = f32[8,64,128]{2,1,0:T(8,128)S(1)} all-to-all(f32[8,64,128]{2,1,0:T(8,128)S(1)} %dynamic-slice_bitcast_fusion), channel_id=1, replica_groups=mesh['dop'=8,'slow'=4] {'dop'}, dimensions={0} | all-to-all | bytes 524288 | tf_op jit(solution)/shard_map/all_to_all | solution.py:162
  115.4 0.7 copy_bitcast_fusion
Async XLA Ops:
  6.5 93.4 %all-reduce.3.cloned.1.call-start = ((), (), s32[]{:S(2)}) async-start(), calls=%async_computation.1 | async-start | bytes 2097152
  8.9 0.9 copy-start.1
  9.8 0.9 copy-start.2
  10.7 0.8 copy-start.3
  11.5 0.8 copy-start.4
  12.4 0.7 copy-start.5
  30.7 31.8 %copy-start.6 = (u32[32]{0:T(128)S(1)}, u32[32]{0:T(128)}, u32[]{:S(2)}) copy-start(u32[32]{0:T(128)} %constant.71) | copy-start | bytes 388
  31.7 16.4 %collective-permute-start = (f32[2048,32]{0,1:T(8,128)}, f32[2048,32]{0,1:T(8,128)S(1)}, u32[]{:S(2)}, u32[]{:S(2)}) collective-permute-start(f32[2048,32]{0,1:T(8,128)} %copy.23), channel_id=1, source_target_pairs={{0,4},{4,8},{8,12},{12,16},{16,20},{20,24},{24,28},{1,5},{5,9},{9,... | collective-permute-start | bytes 786440 | tf_op jit(solution)/shard_map/ppermute | solution.py:149
  36.9 16.8 %collective-permute-start.1 = (f32[2048,32]{0,1:T(8,128)S(1)}, f32[2048,32]{0,1:T(8,128)}, u32[]{:S(2)}, u32[]{:S(2)}) collective-permute-start(f32[2048,32]{0,1:T(8,128)S(1)} %copy.25), channel_id=1, source_target_pairs={{4,0},{8,4},{12,8},{16,12},{20,16},{24,20},{28,24},{5,1},{9,5},{13... | collective-permute-start | bytes 786440 | tf_op jit(solution)/shard_map/ppermute | solution.py:149
  61.4 1.0 copy-start
Sparse Core Ops, SparseCore 0:
  62.6 37.3 all-reduce.2

commit v2 on v1

--- a/solution.py
+++ b/solution.py
@@ -35,13 +35,15 @@
 
 
 def power_kernel(
-    batch_count, total_batches, per_band, scale,
-    order_ref, x_ref, walk_ref, base_cos, base_sin, band_cos, band_sin,
-    own_ref, rim_ref, table, packed, own_sum, rim_sum,
+    batch_count, total_batches, per_band, scale, joined,
+    order_ref, x_ref, walk_ref, turns, *refs,
 ):
+    *outs, table, packed, own_sum, rim_sum = refs
     step = pl.program_id(0)
     short = x_ref.shape[3] // RADIX
     bins = table.shape[1]
+    base_rows = max(per_band, TILE)
+    bands_at = RADIX * base_rows
 
     @pl.when(step == 0)
     def _():
@@ -54,15 +56,15 @@
             start = pl.multiple_of(tile * TILE, TILE)
             first = start // per_band
             inside = pl.multiple_of(start % per_band, TILE) if per_band > TILE else 0
-            vc = band_cos[pl.ds(order_ref[first], 1), :]
-            vs = band_sin[pl.ds(order_ref[first], 1), :]
+            vc = turns[0, pl.ds(bands_at + order_ref[first], 1), :]
+            vs = turns[1, pl.ds(bands_at + order_ref[first], 1), :]
             for extra in range(1, max(1, TILE // per_band)):
                 band = order_ref[first + extra]
-                vc = jnp.where(row == extra, band_cos[pl.ds(band, 1), :], vc)
-                vs = jnp.where(row == extra, band_sin[pl.ds(band, 1), :], vs)
+                vc = jnp.where(row == extra, turns[0, pl.ds(bands_at + band, 1), :], vc)
+                vs = jnp.where(row == extra, turns[1, pl.ds(bands_at + band, 1), :], vs)
             for r in range(RADIX):
-                bc = base_cos[r, pl.ds(inside, TILE), :]
-                bs = base_sin[r, pl.ds(inside, TILE), :]
+                bc = turns[0, pl.ds(r * base_rows + inside, TILE), :]
+                bs = turns[1, pl.ds(r * base_rows + inside, TILE), :]
                 table[r, pl.ds(start, TILE), :short] = (bc * vc - bs * vs).astype(jnp.bfloat16)
                 table[r, pl.ds(start, TILE), short:] = (bs * vc + bc * vs).astype(jnp.bfloat16)
 
@@ -95,12 +97,27 @@
 
     @pl.when(step == batch_count - 1)
     def _():
-        for r in range(RADIX):
-            own_ref[pl.ds(r, bins, stride=RADIX), :] = own_sum[r] * scale
-            rim_ref[pl.ds(r, bins, stride=RADIX), :] = rim_sum[r] * scale
-
-
-def aligned_power(profiles, range_walk, band_order, total_batches):
+        if joined:
+            out_ref = outs[0]
+            band_rows = per_band * RADIX
+            half = band_rows // 2
+
+            @pl.loop(0, bins // per_band)
+            def _(block):
+                rows = pl.ds(pl.multiple_of(block * per_band, per_band), per_band)
+                for r in range(RADIX):
+                    out_ref[block, pl.ds(r, per_band, stride=RADIX), :] = rim_sum[r, rows, :] * scale
+                low, high = out_ref[block, :half, :], out_ref[block, half:band_rows, :]
+                out_ref[block, band_rows:, :] = low + pltpu.roll(high, LANES // 2, 1)
+                for r in range(RADIX):
+                    out_ref[block, pl.ds(r, per_band, stride=RADIX), :] = own_sum[r, rows, :] * scale
+        else:
+            for r in range(RADIX):
+                outs[0][pl.ds(r, bins, stride=RADIX), :] = own_sum[r] * scale
+                outs[1][pl.ds(r, bins, stride=RADIX), :] = rim_sum[r] * scale
+
+
+def aligned_power(profiles, range_walk, band_order, total_batches, joined):
     batch_count, _, delays, pulses = profiles.shape
     band_count = band_order.shape[0]
     band_rows = pulses // band_count
@@ -113,23 +130,26 @@
     walks = jnp.sum(jnp.where(picked, range_walk.reshape(1, band_count, band_rows), 0), axis=1)
     walks = jnp.broadcast_to(walks.reshape(bins, RADIX).T[:, :, None], (RADIX, bins, LANES))
     inner = np.arange(max(per_band, TILE)) % per_band
-    base = rotation(RADIX * inner[None, :] + np.arange(RADIX)[:, None], short, pulses)
-    band = rotation(np.arange(band_count) * band_rows, short, pulses)
+    base = (RADIX * inner[None, :] + np.arange(RADIX)[:, None]).reshape(-1)
+    band = np.arange(band_count) * band_rows
+    turns = np.stack(rotation(np.concatenate([base, band]), short, pulses))
     whole = lambda shape: pl.BlockSpec(shape, lambda g, order: (0,) * len(shape))
-    out = jax.ShapeDtypeStruct((pulses, LANES), jnp.float32)
+    if joined:
+        shapes = ((band_count, band_rows + band_rows // 2, LANES),)
+    else:
+        shapes = ((pulses, LANES),) * 2
     return pl.pallas_call(
-        functools.partial(power_kernel, batch_count, total_batches, per_band, scale),
-        out_shape=(out, out),
+        functools.partial(power_kernel, batch_count, total_batches, per_band, scale, joined),
+        out_shape=[jax.ShapeDtypeStruct(shape, jnp.float32) for shape in shapes],
         grid_spec=pltpu.PrefetchScalarGridSpec(
             num_scalar_prefetch=1,
             grid=(batch_count,),
             in_specs=[
                 pl.BlockSpec((1, 2, LANES, pulses), lambda g, order: (g, 0, 0, 0)),
                 whole(walks.shape),
-                whole(base[0].shape), whole(base[1].shape),
-                whole(band[0].shape), whole(band[1].shape),
+                whole(turns.shape),
             ],
-            out_specs=(whole(out.shape), whole(out.shape)),
+            out_specs=[whole(shape) for shape in shapes],
             scratch_shapes=[
                 pltpu.VMEM((RADIX, bins, 2 * short), jnp.bfloat16),
                 pltpu.VMEM((RADIX, 2 * LANES, 2 * short), jnp.bfloat16),
@@ -140,7 +160,118 @@
         compiler_params=pltpu.CompilerParams(
             dimension_semantics=("arbitrary",), vmem_limit_bytes=48 << 20
         ),
-    )(band_order, profiles, walks, *(jnp.asarray(part) for part in (*base, *band)))
+    )(band_order, profiles, walks, jnp.asarray(turns))
+
+
+MESH = pl.DeviceIdType.MESH
+
+
+def bit_of(value, k):
+    return lax.rem(lax.div(value, 1 << k), 2)
+
+
+def flipped(value, mask):
+    result = value
+    for k in range(mask.bit_length()):
+        if mask >> k & 1:
+            result = result + (1 << k) * (1 - 2 * bit_of(value, k))
+    return result
+
+
+def regroup_kernel(dop_count, slow_count, data, out_ref, *refs):
+    levels = slow_count.bit_length() - 1
+    kept, arrived = refs[:levels], refs[levels:2 * levels]
+    landed, send_sem, recv_sem = refs[2 * levels:]
+    dop, slow = lax.axis_index("dop"), lax.axis_index("slow")
+    band_rows = out_ref.shape[0]
+    partners = [(dop, flipped(slow, 1 << k)) for k in range(levels)]
+    partners += [(flipped(dop, j), slow) for j in range(1, dop_count)]
+
+    barrier = pltpu.get_barrier_semaphore()
+    for partner in partners:
+        pl.semaphore_signal(barrier, inc=1, device_id=partner, device_id_type=MESH)
+    pl.semaphore_wait(barrier, len(partners))
+
+    order = list(range(dop_count - 1, -1, -1))
+    copies = {}
+
+    def send(level, j, source, target, device):
+        copies[level, j] = pltpu.make_async_remote_copy(
+            src_ref=source, dst_ref=target,
+            send_sem=send_sem.at[level, j], recv_sem=recv_sem.at[level, j],
+            device_id=device, device_id_type=MESH,
+        )
+        copies[level, j].start()
+
+    for j in order:
+        send(0, j, data.at[flipped(dop, j), :, 1 - bit_of(slow, 0)], arrived[0].at[j], partners[0])
+    for level in range(levels):
+        for j in order:
+            copies[level, j].wait_recv()
+            bit = bit_of(slow, level)
+            held = data[flipped(dop, j), :, bit] if level == 0 else kept[level - 1][j, :, bit]
+            total = held + arrived[level][j]
+            if level < levels - 1:
+                kept[level][j] = total.reshape(kept[level].shape[1:])
+                send(
+                    level + 1, j, kept[level].at[j, :, 1 - bit_of(slow, level + 1)],
+                    arrived[level + 1].at[j], partners[level + 1],
+                )
+            elif j:
+                kept[level][j] = total[0]
+                send(levels, j, kept[level].at[j], landed.at[j], (flipped(dop, j), slow))
+            else:
+                landed[0] = total[0]
+    for j in order[:-1]:
+        copies[levels, j].wait_recv()
+
+    half = band_rows // 2
+    lane = lax.broadcasted_iota(jnp.int32, (half, LANES), 1)
+    for e in range(dop_count):
+        main = landed[flipped(dop, e), :band_rows, :]
+        low = jnp.zeros((half, LANES), jnp.float32)
+        high = low
+        for source, mine in ((e - 1, lane < WALK), (e + 1, lane >= LANES - WALK)):
+            if 0 <= source < dop_count:
+                rim = landed[flipped(dop, source), band_rows:, :]
+                low += jnp.where(mine, rim, 0.0)
+                high += jnp.where(mine, pltpu.roll(rim, LANES // 2, 1), 0.0)
+        out_ref[:half, e * LANES:(e + 1) * LANES] = main[:half] + low
+        out_ref[half:, e * LANES:(e + 1) * LANES] = main[half:] + high
+    for copy in copies.values():
+        copy.wait_send()
+
+
+def regroup(blocks, dop_count, slow_count):
+    rows = blocks.shape[1]
+    band_rows = rows // 3 * 2
+    levels = slow_count.bit_length() - 1
+    kept, arrived = [], []
+    count = slow_count
+    for level in range(levels):
+        count //= 2
+        pair = (count // 2, 2) if count > 1 else ()
+        kept.append(pltpu.VMEM((dop_count, *pair, rows, LANES), jnp.float32))
+        arrived.append(pltpu.VMEM((dop_count, count, rows, LANES), jnp.float32))
+    return pl.pallas_call(
+        functools.partial(regroup_kernel, dop_count, slow_count),
+        out_shape=jax.ShapeDtypeStruct((band_rows, dop_count * LANES), jnp.float32),
+        in_specs=[pl.BlockSpec(memory_space=pltpu.VMEM)],
+        out_specs=pl.BlockSpec(memory_space=pltpu.VMEM),
+        scratch_shapes=[
+            *kept, *arrived,
+            pltpu.VMEM((dop_count, rows, LANES), jnp.float32),
+            pltpu.SemaphoreType.DMA((levels + 1, dop_count)),
+            pltpu.SemaphoreType.DMA((levels + 1, dop_count)),
+        ],
+        compiler_params=pltpu.CompilerParams(
+            collective_id=0, has_side_effects=True, vmem_limit_bytes=32 << 20
+        ),
+    )(blocks.reshape(dop_count, slow_count // 2, 2, rows, LANES))
+
+
+def power_of_two(count):
+    return count & (count - 1) == 0
 
 
 def neighbours(value, steps):
@@ -166,8 +297,16 @@
 def on_device(profiles, range_walk, band_order):
     total_batches = profiles.shape[0] * lax.axis_size("slow")
     delays = profiles.shape[2]
-    own, rim = aligned_power(profiles, range_walk, band_order, total_batches)
-    return exchange(own, rim, delays)
+    dop_count, slow_count = lax.axis_size("dop"), lax.axis_size("slow")
+    per_band = profiles.shape[3] // (dop_count * slow_count * RADIX)
+    joined = (
+        delays == LANES and per_band % TILE == 0 and slow_count > 1
+        and power_of_two(dop_count) and power_of_two(slow_count)
+    )
+    sums = aligned_power(profiles, range_walk, band_order, total_batches, joined)
+    if joined:
+        return regroup(sums[0], dop_count, slow_count)
+    return exchange(*sums, delays)
 
 
 def solution(mesh):

time: 123 us -> 45.8 us (0.37)
  waiting for transfers between devices: 46.2 us -> 0 us
  Pallas kernels: 17.3 us -> 40.9 us
  local copies, waits for them, and re-layouts: 23.3 us -> 3.73 us
  blocking collectives: 13.8 us -> 0 us
  between operations: 13.5 us -> 0.04 us
  starting transfers between devices: 6.2 us -> 0 us
  other arithmetic: 2.68 us -> 0.95 us
    unnamed x2 -> x0, waiting for transfers between devices: 36.9 us -> none
    pallas_call x0 -> x1, Pallas kernels: none -> 21.4 us  [regroup(): pl.pallas_call(functools.partial(regroup_kernel, dop_count, slow_count),...]
    all_to_all x1 -> x0, blocking collectives: 13.8 us -> none  [exchange(): lax.all_to_all(summed, 'dop', split_axis=0, concat_axis=0, tiled=True)]
    scatter-add x2 -> x0, local copies, waits for them, and re-layouts: 10.6 us -> none  [the longest x1 6.08 us: exchange(): own = own.at[:, delays - WALK:].add(from_above)]
    ppermute x2 -> x0, waiting for transfers between devices: 9.21 us -> none  [neighbours(): return lax.ppermute(value, 'dop', pairs)]
    ppermute x2 -> x0, starting transfers between devices: 6.19 us -> none  [neighbours(): return lax.ppermute(value, 'dop', pairs)]
    unnamed x15 -> x5, local copies, waits for them, and re-layouts: 5.75 us -> 2.35 us
    pallas_call x1, Pallas kernels: 17.3 us -> 19.5 us  [aligned_power(): pl.pallas_call(functools.partial(power_kernel, batch_count, total_batches...]
  transfers between devices with their start and end apart: 3 -> 0, of which waited for: 2 -> 0; matrix products, arithmetic and copies ran while one was open for 6% -> 0% of each run, Pallas kernels for 0% -> 0%
where the time goes in v2:
time: 45.8 us; the launch traced here: 45.6 us
  Pallas kernels  40.9 us (89%)
  local copies, waits for them, and re-layouts  3.73 us (8%)
  other arithmetic  0.95 us (2%)
    pallas_call x1, Pallas kernels, regroup(): pl.pallas_call(functools.partial(regroup_kernel, dop_count, slow_count),...  21.4 us
    pallas_call x1, Pallas kernels, aligned_power(): pl.pallas_call(functools.partial(power_kernel, batch_count, total_batches...  19.5 us
    unnamed x5, local copies, waits for them, and re-layouts  2.35 us

profile of v2, /device:TPU:0, one launch (start us, length us, event | category | flops | bytes accessed | tf_op | source)
XLA Modules:
  0.0 45.6 jit_solution(1741285079235269642)
XLA Ops:
  0.0 0.7 %iota_compare_fusion = pred[32,32]{1,0:T(8,128)(4,1)S(1)} fusion(s32[32]{0:T(128)} %order_ref.1), kind=kLoop, calls=%fused_computation.1 | loop fusion | flops 1024 | bytes 1152 | tf_op jit(solution)/shard_map/eq | solution.py:129
  0.7 0.8 %broadcast_in_dim.31 = s32[32,64]{1,0:T(8,128)S(1)} reshape(s32[2048]{0:T(1024)} %param.5) | data formatting | bytes 16384 | tf_op jit(solution)/shard_map/jit(_where)/broadcast_in_dim | solution.py:130
  1.5 0.2 select_reduce_fusion
  1.7 0.2 reshape.34
  1.9 0.1 copy.6
  2.0 0.3 broadcast_in_dim.34.walk_ref
  2.3 0.0 copy-start
  2.4 1.0 %copy-done = f32[2,96,512]{2,1,0:T(8,128)S(1)} copy-done((f32[2,96,512]{2,1,0:T(8,128)S(1)}, f32[2,96,512]{2,1,0:T(8,128)}, u32[]{:S(2)}) %copy-start) | copy-done | bytes 393240
  3.3 0.0 copy-start.1
  3.3 0.7 %copy-done.1 = s32[32]{0:T(128)S(1)} copy-done((s32[32]{0:T(128)S(1)}, s32[32]{0:T(128)}, u32[]{:S(2)}) %copy-start.1) | copy-done | bytes 152
  4.0 19.5 %shard_map.46 = f32[32,96,128]{2,1,0:T(8,128)S(1)} custom-call(s32[32]{0:T(128)S(1)} %copy-done.1, bf16[8,2,128,2048]{3,2,1,0:T(8,128)(2,1)} %x_ref.1, s32[4,512,128]{2,1,0:T(8,128)S(1)} %broadcast_in_dim.34.walk_ref, f32[2,96,512]{2,1,0:T(8,128)S(1)} %copy-done), custom_call_target="tpu_custom_call" | custom-call | tf_op jit(solution)/shard_map/pallas_call | solution.py:141
  23.5 21.4 %shard_map.47 = f32[64,1024]{1,0:T(8,128)S(1)} custom-call(f32[8,2,2,96,128]{4,3,2,1,0:T(8,128)S(1)} %bitcast.2), custom_call_target="tpu_custom_call" | custom-call | tf_op jit(solution)/shard_map/pallas_call | solution.py:256
  44.9 0.7 %copy.8 = f32[64,1024]{1,0:T(8,128)} copy(f32[64,1024]{1,0:T(8,128)S(1)} %shard_map.47) | data formatting | bytes 524288
Async XLA Ops:
  2.3 1.0 %copy-start = (f32[2,96,512]{2,1,0:T(8,128)S(1)}, f32[2,96,512]{2,1,0:T(8,128)}, u32[]{:S(2)}) copy-start(f32[2,96,512]{2,1,0:T(8,128)} %constant.4.clone.turns) | copy-start | bytes 1179652
  3.3 0.7 %copy-start.1 = (s32[32]{0:T(128)S(1)}, s32[32]{0:T(128)}, u32[]{:S(2)}) copy-start(s32[32]{0:T(128)} %order_ref.1) | copy-start | bytes 388

commit v3 on v2

--- a/solution.py
+++ b/solution.py
@@ -21,9 +21,9 @@
     return np.cos(angles).astype(np.float32), np.sin(angles).astype(np.float32)
 
 
-def quarter_sums(x_ref, short):
-    re = [x_ref[0, 0, :, q * short:(q + 1) * short].astype(jnp.float32) for q in range(RADIX)]
-    im = [x_ref[0, 1, :, q * short:(q + 1) * short].astype(jnp.float32) for q in range(RADIX)]
+def quarter_sums(x_ref, at, short):
+    re = [x_ref[at, 0, :, q * short:(q + 1) * short].astype(jnp.float32) for q in range(RADIX)]
+    im = [x_ref[at, 1, :, q * short:(q + 1) * short].astype(jnp.float32) for q in range(RADIX)]
     are, aim, bre, bim = re[0] + re[2], im[0] + im[2], re[0] - re[2], im[0] - im[2]
     cre, cim, dre, dim = re[1] + re[3], im[1] + im[3], re[1] - re[3], im[1] - im[3]
     return (
@@ -38,7 +38,7 @@
     batch_count, total_batches, per_band, scale, joined,
     order_ref, x_ref, walk_ref, turns, *refs,
 ):
-    *outs, table, packed, own_sum, rim_sum = refs
+    *outs, table, packed, own_sum, rim_sum, walks = refs
     step = pl.program_id(0)
     short = x_ref.shape[3] // RADIX
     bins = table.shape[1]
@@ -63,39 +63,59 @@
                 vc = jnp.where(row == extra, turns[0, pl.ds(bands_at + band, 1), :], vc)
                 vs = jnp.where(row == extra, turns[1, pl.ds(bands_at + band, 1), :], vs)
             for r in range(RADIX):
+                if joined:
+                    at = order_ref[first] * (per_band * RADIX) + inside * RADIX + r
+                    walks[r, pl.ds(start, TILE), :] = walk_ref[pl.ds(at, TILE, stride=RADIX), :]
+                else:
+                    walks[r, pl.ds(start, TILE), :] = walk_ref[r, pl.ds(start, TILE), :]
                 bc = turns[0, pl.ds(r * base_rows + inside, TILE), :]
                 bs = turns[1, pl.ds(r * base_rows + inside, TILE), :]
                 table[r, pl.ds(start, TILE), :short] = (bc * vc - bs * vs).astype(jnp.bfloat16)
                 table[r, pl.ds(start, TILE), short:] = (bs * vc + bc * vs).astype(jnp.bfloat16)
 
-    batch = lax.axis_index("slow") * batch_count + step
+    each = x_ref.shape[0]
+    batch = lax.axis_index("slow") * batch_count + step * each
     lane = lax.broadcasted_iota(jnp.int32, (bins, LANES), 1)
-    sums = quarter_sums(x_ref, short)
-    for r in range(RADIX):
-        yre, yim = (part.astype(jnp.bfloat16) for part in sums[r])
-        packed[r, :LANES, :short] = yre
-        packed[r, :LANES, short:] = yim
-        packed[r, LANES:, :short] = yim
-        packed[r, LANES:, short:] = -yre
+    for at in range(each):
+        top, low = 2 * LANES * at, 2 * LANES * at + LANES
+        for r, parts in enumerate(quarter_sums(x_ref, at, short)):
+            yre, yim = (part.astype(jnp.bfloat16) for part in parts)
+            packed[r, top:low, :short] = yre
+            packed[r, top:low, short:] = yim
+            packed[r, low:low + LANES, :short] = yim
+            packed[r, low:low + LANES, short:] = -yre
+
+    def align(r, spec):
+        own_add, rim_add = 0.0, 0.0
+        for at in range(each):
+            re = spec[:, 2 * LANES * at:2 * LANES * at + LANES]
+            im = spec[:, 2 * LANES * at + LANES:2 * LANES * (at + 1)]
+            power = re * re + im * im
+            moved = walks[r] * (batch + at)
+            if power_of_two(total_batches):
+                offset = lax.shift_right_arithmetic(moved, total_batches.bit_length() - 1)
+            else:
+                offset = jnp.floor_divide(moved, total_batches)
+            source = lane + offset
+            wrapped = source & (LANES - 1)
+            value = jnp.take_along_axis(power, wrapped, axis=1, mode="promise_in_bounds")
+            inside = source == wrapped
+            own_add += jnp.where(inside, value, 0.0)
+            rim_add += jnp.where(inside, 0.0, value)
+        own_sum[r] += own_add
+        rim_sum[r] += rim_add
+
+    pending = None
     for r in range(RADIX):
         spec = lax.dot_general(
             table[r], packed[r], (((1,), (1,)), ((), ())), preferred_element_type=jnp.float32
         )
-        re, im = spec[:, :LANES], spec[:, LANES:]
-        power = re * re + im * im
-        moved = walk_ref[r] * batch
-        if total_batches & (total_batches - 1) == 0:
-            offset = lax.shift_right_arithmetic(moved, total_batches.bit_length() - 1)
-        else:
-            offset = jnp.floor_divide(moved, total_batches)
-        source = lane + offset
-        wrapped = source & (LANES - 1)
-        value = jnp.take_along_axis(power, wrapped, axis=1, mode="promise_in_bounds")
-        inside = source == wrapped
-        own_sum[r] += jnp.where(inside, value, 0.0)
-        rim_sum[r] += jnp.where(inside, 0.0, value)
-
-    @pl.when(step == batch_count - 1)
+        if pending is not None:
+            align(r - 1, pending)
+        pending = spec
+    align(RADIX - 1, pending)
+
+    @pl.when(step == pl.num_programs(0) - 1)
     def _():
         if joined:
             out_ref = outs[0]
@@ -126,9 +146,13 @@
     scale = 1.0 / (total_batches * pulses)
     if delays < LANES:
         profiles = jnp.pad(profiles, ((0, 0), (0, 0), (0, LANES - delays), (0, 0)))
-    picked = band_order[:, None, None] == jnp.arange(band_count, dtype=jnp.int32)[None, :, None]
-    walks = jnp.sum(jnp.where(picked, range_walk.reshape(1, band_count, band_rows), 0), axis=1)
-    walks = jnp.broadcast_to(walks.reshape(bins, RADIX).T[:, :, None], (RADIX, bins, LANES))
+    if joined:
+        walks = jnp.broadcast_to(range_walk[:, None], (pulses, LANES))
+    else:
+        picked = band_order[:, None, None] == jnp.arange(band_count, dtype=jnp.int32)[None, :, None]
+        walks = jnp.sum(jnp.where(picked, range_walk.reshape(1, band_count, band_rows), 0), axis=1)
+        walks = jnp.broadcast_to(walks.reshape(bins, RADIX).T[:, :, None], (RADIX, bins, LANES))
+    each = 2 if batch_count % 2 == 0 else 1
     inner = np.arange(max(per_band, TILE)) % per_band
     base = (RADIX * inner[None, :] + np.arange(RADIX)[:, None]).reshape(-1)
     band = np.arange(band_count) * band_rows
@@ -143,18 +167,19 @@
         out_shape=[jax.ShapeDtypeStruct(shape, jnp.float32) for shape in shapes],
         grid_spec=pltpu.PrefetchScalarGridSpec(
             num_scalar_prefetch=1,
-            grid=(batch_count,),
+            grid=(batch_count // each,),
             in_specs=[
-                pl.BlockSpec((1, 2, LANES, pulses), lambda g, order: (g, 0, 0, 0)),
+                pl.BlockSpec((each, 2, LANES, pulses), lambda g, order: (g, 0, 0, 0)),
                 whole(walks.shape),
                 whole(turns.shape),
             ],
             out_specs=[whole(shape) for shape in shapes],
             scratch_shapes=[
                 pltpu.VMEM((RADIX, bins, 2 * short), jnp.bfloat16),
-                pltpu.VMEM((RADIX, 2 * LANES, 2 * short), jnp.bfloat16),
+                pltpu.VMEM((RADIX, 2 * LANES * each, 2 * short), jnp.bfloat16),
                 pltpu.VMEM((RADIX, bins, LANES), jnp.float32),
                 pltpu.VMEM((RADIX, bins, LANES), jnp.float32),
+                pltpu.VMEM((RADIX, bins, LANES), jnp.int32),
             ],
         ),
         compiler_params=pltpu.CompilerParams(

time: 45.8 us -> 43 us (0.939)
  Pallas kernels: 40.9 us -> 39.4 us
  other arithmetic: 0.95 us -> 0 us
    pallas_call x1, Pallas kernels: 19.5 us -> 18.1 us  [aligned_power(): pl.pallas_call(functools.partial(power_kernel, batch_count, total_batches...]
    eq x1 -> x0, other arithmetic: 0.73 us -> none  [aligned_power(): band_order[:, None, None]]
    broadcast_in_dim x2 -> x1, local copies, waits for them, and re-layouts: 1.1 us -> 1.02 us  [aligned_power(): walks = jnp.broadcast_to(range_walk[:, None], (pulses, LANES))]
where the time goes in v3:
time: 43 us; the launch traced here: 42.8 us
  Pallas kernels  39.4 us (92%)
  local copies, waits for them, and re-layouts  3.37 us (8%)
    pallas_call x1, Pallas kernels, regroup(): pl.pallas_call(functools.partial(regroup_kernel, dop_count, slow_count),...  21.4 us
    pallas_call x1, Pallas kernels, aligned_power(): pl.pallas_call(functools.partial(power_kernel, batch_count, total_batches...  18.1 us
    unnamed x5, local copies, waits for them, and re-layouts  2.35 us
    broadcast_in_dim x1, local copies, waits for them, and re-layouts, aligned_power(): walks = jnp.broadcast_to(range_walk[:, None], (pulses, LANES))  1.02 us

profile of v3, /device:TPU:0, one launch (start us, length us, event | category | flops | bytes accessed | tf_op | source)
XLA Modules:
  0.0 42.8 jit_solution(11370458590853907184)
XLA Ops:
  0.0 1.0 %broadcast_in_dim.2.walk_ref = s32[2048,128]{1,0:T(8,128)S(1)} broadcast(s32[2048]{0:T(1024)} %param.5), dimensions={0} | broadcast | bytes 1056768 | tf_op jit(solution)/shard_map/broadcast_in_dim | solution.py:150
  1.0 0.0 copy-start
  1.0 1.0 %copy-done = f32[2,96,512]{2,1,0:T(8,128)S(1)} copy-done((f32[2,96,512]{2,1,0:T(8,128)S(1)}, f32[2,96,512]{2,1,0:T(8,128)}, u32[]{:S(2)}) %copy-start) | copy-done | bytes 393240
  2.0 0.0 copy-start.1
  2.0 0.7 %copy-done.1 = s32[32]{0:T(128)S(1)} copy-done((s32[32]{0:T(128)S(1)}, s32[32]{0:T(128)}, u32[]{:S(2)}) %copy-start.1) | copy-done | bytes 152
  2.7 18.1 %shard_map.46 = f32[32,96,128]{2,1,0:T(8,128)S(1)} custom-call(s32[32]{0:T(128)S(1)} %copy-done.1, bf16[8,2,128,2048]{3,2,1,0:T(8,128)(2,1)} %x_ref.1, s32[2048,128]{1,0:T(8,128)S(1)} %broadcast_in_dim.2.walk_ref, f32[2,96,512]{2,1,0:T(8,128)S(1)} %copy-done), custom_call_target="tpu_custom_call" | custom-call | tf_op jit(solution)/shard_map/pallas_call | solution.py:165
  20.8 21.4 %shard_map.47 = f32[64,1024]{1,0:T(8,128)S(1)} custom-call(f32[8,2,2,96,128]{4,3,2,1,0:T(8,128)S(1)} %bitcast.1), custom_call_target="tpu_custom_call" | custom-call | tf_op jit(solution)/shard_map/pallas_call | solution.py:281
  42.1 0.7 %copy.6 = f32[64,1024]{1,0:T(8,128)} copy(f32[64,1024]{1,0:T(8,128)S(1)} %shard_map.47) | data formatting | bytes 524288
Async XLA Ops:
  1.0 1.0 %copy-start = (f32[2,96,512]{2,1,0:T(8,128)S(1)}, f32[2,96,512]{2,1,0:T(8,128)}, u32[]{:S(2)}) copy-start(f32[2,96,512]{2,1,0:T(8,128)} %constant.2.clone.turns) | copy-start | bytes 1179652
  2.0 0.7 %copy-start.1 = (s32[32]{0:T(128)S(1)}, s32[32]{0:T(128)}, u32[]{:S(2)}) copy-start(s32[32]{0:T(128)} %order_ref.1) | copy-start | bytes 388

commit v4 on v3

--- a/solution.py
+++ b/solution.py
@@ -183,7 +183,7 @@
             ],
         ),
         compiler_params=pltpu.CompilerParams(
-            dimension_semantics=("arbitrary",), vmem_limit_bytes=48 << 20
+            dimension_semantics=("arbitrary",), vmem_limit_bytes=60 << 20
         ),
     )(band_order, profiles, walks, jnp.asarray(turns))
 

time: 43 us -> 45.4 us (1.056)
  Pallas kernels: 39.4 us -> 41 us
  local copies, waits for them, and re-layouts: 3.37 us -> 4.12 us
    pallas_call x1, Pallas kernels: 18.1 us -> 19.7 us  [aligned_power(): pl.pallas_call(functools.partial(power_kernel, batch_count, total_batches...]
    broadcast_in_dim x1, local copies, waits for them, and re-layouts: 1.02 us -> 2.01 us  [aligned_power(): walks = jnp.broadcast_to(range_walk[:, None], (pulses, LANES))]
    unnamed x5 -> x3, local copies, waits for them, and re-layouts: 2.35 us -> 2.11 us
where the time goes in v4:
time: 45.4 us; the launch traced here: 45.2 us
  Pallas kernels  41 us (90%)
  local copies, waits for them, and re-layouts  4.12 us (9%)
    pallas_call x1, Pallas kernels, regroup(): pl.pallas_call(functools.partial(regroup_kernel, dop_count, slow_count),...  21.3 us
    pallas_call x1, Pallas kernels, aligned_power(): pl.pallas_call(functools.partial(power_kernel, batch_count, total_batches...  19.7 us
    unnamed x3, local copies, waits for them, and re-layouts  2.11 us
    broadcast_in_dim x1, local copies, waits for them, and re-layouts, aligned_power(): walks = jnp.broadcast_to(range_walk[:, None], (pulses, LANES))  2.01 us

profile of v4, /device:TPU:0, one launch (start us, length us, event | category | flops | bytes accessed | tf_op | source)
XLA Modules:
  0.0 45.2 jit_solution(7753229618567127334)
XLA Ops:
  0.0 2.0 %broadcast_in_dim.2.walk_ref = s32[2048,128]{1,0:T(8,128)} broadcast(s32[2048]{0:T(1024)} %param.5), dimensions={0} | broadcast | bytes 1056768 | tf_op jit(solution)/shard_map/broadcast_in_dim | solution.py:150
  2.0 19.7 %shard_map.46 = f32[32,96,128]{2,1,0:T(8,128)} custom-call(s32[32]{0:T(128)} %order_ref.1, bf16[8,2,128,2048]{3,2,1,0:T(8,128)(2,1)} %x_ref.1, s32[2048,128]{1,0:T(8,128)} %broadcast_in_dim.2.walk_ref, f32[2,96,512]{2,1,0:T(8,128)} %constant.2.clone.turns), custom_call_target="tpu_custom_call" | custom-call | tf_op jit(solution)/shard_map/pallas_call | solution.py:165
  21.7 0.0 copy-start
  21.7 1.4 %copy-done = f32[32,96,128]{2,1,0:T(8,128)S(1)} copy-done((f32[32,96,128]{2,1,0:T(8,128)S(1)}, f32[32,96,128]{2,1,0:T(8,128)}, u32[]{:S(2)}) %copy-start) | copy-done | bytes 1572888
  23.2 21.3 %shard_map.47 = f32[64,1024]{1,0:T(8,128)S(1)} custom-call(f32[8,2,2,96,128]{4,3,2,1,0:T(8,128)S(1)} %bitcast.1), custom_call_target="tpu_custom_call" | custom-call | tf_op jit(solution)/shard_map/pallas_call | solution.py:281
  44.5 0.7 %copy.6 = f32[64,1024]{1,0:T(8,128)} copy(f32[64,1024]{1,0:T(8,128)S(1)} %shard_map.47) | data formatting | bytes 524288
Async XLA Ops:
  21.7 1.4 %copy-start = (f32[32,96,128]{2,1,0:T(8,128)S(1)}, f32[32,96,128]{2,1,0:T(8,128)}, u32[]{:S(2)}) copy-start(f32[32,96,128]{2,1,0:T(8,128)} %shard_map.46) | copy-start | bytes 4718596
